TPU v7x, 32 devices: a whole 2x2x4 slice. The times are simulated.
32 devices in a mesh: grp: 2 (over core), dev: 16 (over z, y, x).
Axes of the slice: x: 2, y: 2, z: 4, core: 2. Of those that a mesh axis runs over, the one named last changes fastest.
Arguments:
- accum: float32 [4096, 24, 128], P(('grp', 'dev')), may hold values from -48 to 48
- step_count: int32 [24], replicated, may hold values from 1 to 12
- stretch_slot: int32 [4096], replicated, may hold values from 0 to 4095, as said below
- span_length: int32 [32], replicated, may hold values from 1 to 256, 4096 in all
- wet_mask: int32 [8192], P(('grp', 'dev')), may hold values 0 or 1
Outputs:
- ocean_flux: float32 [8192, 24, 128], P(('grp', 'dev'))
Inputs may be any that keep to these rules, and one draw needn't show every extreme that they name: `stretch_slot`: A permutation of the slots; any 32 consecutive row blocks lie on 32 different atmosphere devices (slot // 128). `span_length`: sums to 4096; some ocean device owns exactly 256 blocks. `wet_mask`: entries of slots beyond an ocean device's span are ignored.
All inputs are finite; a program needn't handle non-finite values.
Results may differ from a plain program's by a relative error of at most 0.000071.
Values sent between devices are 32-bit elements; how exact they have to be, the bound alone decides.
No kernel may reach another device: no remote copies, remote signals or barrier semaphores. Data moves between devices by JAX's collectives and lax.ppermute only.
A program may use at most 64 MiB of HBM per device.

v0:
```python
import jax
import jax.numpy as jnp
from jax import lax
from jax.sharding import PartitionSpec as P


def passed_along(value, axis, steps):
    count = lax.axis_size(axis)
    initial, last = (max(0, -steps), min(count, count - steps))
    return lax.ppermute(value, axis, [(source, source + steps) for source in range(initial, last)])


def select_rows(picks, table):
    return jnp.dot(
        picks, table, precision=lax.Precision.HIGHEST, preferred_element_type=jnp.float32
    )


def on_device(accum, step_count, stretch_slot, span_length, wet_mask):
    devices = lax.axis_size(("grp", "dev"))
    my_index = lax.axis_index(("grp", "dev"))
    blocks_dev = accum.shape[0]
    fields = accum.shape[1]
    cells = accum.shape[2]
    capacity = wet_mask.shape[0]
    pair_most = capacity // devices
    all_blocks = stretch_slot.shape[0]
    span_end = jnp.cumsum(span_length)
    span_start = span_end - span_length
    all_ids = jnp.arange(all_blocks, dtype=jnp.int32)
    local_ids = jnp.arange(blocks_dev, dtype=jnp.int32)
    mine = stretch_slot[None, :] == (my_index * blocks_dev + local_ids)[:, None]
    my_global = jnp.sum(jnp.where(mine, all_ids[None, :], 0), axis=1)
    owner = jnp.sum((span_end[None, :] <= my_global[:, None]).astype(jnp.int32), axis=1)
    same_owner = owner[:, None] == owner[None, :]
    earlier = my_global[None, :] < my_global[:, None]
    order_in = jnp.sum((same_owner & earlier).astype(jnp.int32), axis=1)
    position = owner * pair_most + order_in
    buffer_ids = jnp.arange(devices * pair_most, dtype=jnp.int32)
    send_picks = (position[None, :] == buffer_ids[:, None]).astype(jnp.float32)
    counts = step_count.astype(jnp.float32)
    normal = (accum / counts[None, :, None]).reshape(blocks_dev, fields * cells)
    sendbuf = select_rows(send_picks, normal).reshape(devices, pair_most, fields, cells)
    received = lax.all_to_all(sendbuf, ("grp", "dev"), split_axis=0, concat_axis=0, tiled=True)
    received = received.reshape(devices * pair_most, fields * cells)
    length = span_length[my_index]
    start = span_start[my_index]
    slots = jnp.arange(capacity, dtype=jnp.int32)
    valid = slots < length
    global_ids = jnp.minimum(start + slots, all_blocks - 1)
    sender = stretch_slot[global_ids] // blocks_dev
    same_sender = (sender[:, None] == sender[None, :]) & valid[None, :]
    lower = slots[None, :] < slots[:, None]
    rank_in = jnp.sum((same_sender & lower).astype(jnp.int32), axis=1)
    place_ids = sender * pair_most + rank_in
    place_picks = (place_ids[:, None] == buffer_ids[None, :]).astype(jnp.float32)
    placed = select_rows(place_picks, received).reshape(capacity, fields, cells)
    wet = (valid & (wet_mask == 1)).astype(jnp.float32)
    masked = placed * wet[:, None, None]
    last_cells = masked[:, :, cells - 1]
    first_cells = masked[:, :, 0]
    last_cell = lax.dynamic_index_in_dim(last_cells, length - 1, 0, keepdims=False)
    first_cell = first_cells[0]
    left_in = passed_along(last_cell, ("grp", "dev"), 1)
    right_in = passed_along(first_cell, ("grp", "dev"), -1)
    before_col = jnp.concatenate([left_in[None, :], last_cells[:-1]], axis=0)
    after_col = jnp.concatenate([first_cells[1:], jnp.zeros((1, fields), jnp.float32)], axis=0)
    after_col = jnp.where((slots == length - 1)[:, None], right_in[None, :], after_col)
    cell_ids = jnp.arange(cells, dtype=jnp.int32)
    distance = jnp.abs(cell_ids[:, None] - cell_ids[None, :])
    stencil = jnp.where(distance == 0, 0.5, jnp.where(distance == 1, 0.25, 0.0)).astype(jnp.float32)
    inner = jnp.dot(
        masked.reshape(capacity * fields, cells),
        stencil,
        precision=lax.Precision.HIGHEST,
        preferred_element_type=jnp.float32,
    ).reshape(capacity, fields, cells)
    first_hot = (cell_ids == 0).astype(jnp.float32)
    last_hot = (cell_ids == cells - 1).astype(jnp.float32)
    edges_added = (
        0.25 * before_col[:, :, None] * first_hot[None, None, :]
        + 0.25 * after_col[:, :, None] * last_hot[None, None, :]
    )
    smoothed = (inner + edges_added) * wet[:, None, None]
    return smoothed


def solution(mesh):
    return jax.shard_map(
        on_device,
        mesh=mesh,
        in_specs=(P(("grp", "dev"), None, None), P(), P(), P(), P(("grp", "dev"))),
        out_specs=P(("grp", "dev"), None, None),
        check_vma=False,
    )
```

profile of v0, /device:TPU:1, one launch (start us, length us, event | category | flops | bytes accessed | tf_op | source)
XLA Modules:
  0.0 114.0 jit_solution(1477209370959415454)
XLA Ops:
  0.0 0.7 convert_element_type.34
  0.7 0.7 copy.21
  1.4 0.1 reduce-window.8
  1.5 0.1 reduce
  1.6 1.1 select_reduce_fusion
  2.7 0.1 convert_reduce_fusion.2
  2.8 0.2 convert_reduce_fusion.1
  3.0 1.6 %broadcast_divide_fusion = f32[128,24,128]{2,1,0:T(8,128)S(1)} fusion(f32[128,24,128]{2,1,0:T(8,128)} %param.5, f32[24]{0:T(128)S(1)} %convert_element_type.34), kind=kLoop, calls=%fused_computation.5 | loop fusion | flops 393216 | bytes 3145824 | tf_op jit(solution)/shard_map/div | solution.py:42
  4.6 0.3 copy.38
  4.9 0.5 copy.22
  5.4 3.1 %fusion.4 = f32[32,8,24,128]{3,1,2,0:T(8,128)} fusion(f32[24,128,128,1]{2,1,0,3:T(8,128)S(1)} %bitcast.43, s32[32,8]{1,0:T(8,128)S(1)} %multiply_add_fusion, s32[128]{0:T(128)S(1)} %multiply_add_fusion.2), kind=kOutput, calls=%fused_computation.12 | convolution fusion | flops 1207992320 | bytes 4720128 | tf_op jit(solution)/shard_map/dot_general | solution.py:14
  8.5 0.0 copy-start.2
  8.5 0.0 copy-start
  8.5 0.0 copy-start.1
  8.5 7.1 %all-to-all-start = ((f32[32,8,24,128]{3,1,2,0:T(8,128)}), f32[32,8,24,128]{3,1,2,0:T(8,128)S(1)}, u32[]{:S(2)}, u32[]{:S(2)}) async-start(f32[32,8,24,128]{3,1,2,0:T(8,128)} %fusion.4), calls=%async_computation | async-start | bytes 6291456 | tf_op jit(solution)/shard_map/all_to_all | solution.py:44
  15.6 0.0 copy-done.2
  15.6 0.7 dynamic_slice.11
  17.6 0.6 dynamic_slice.10
  18.2 0.6 compare_select_fusion
  18.8 0.0 copy-done
  18.8 1.7 %gather_fusion = s32[256]{0:T(256)S(1)} fusion(s32[4096]{0:T(1024)S(1)} %copy-done, s32[1024]{0:T(1024)S(1)} %pad_clamp_fusion), kind=kCustom, calls=%fused_computation | custom fusion | bytes 3072 | tf_op jit(solution)/shard_map/gather | solution.py:51
  20.6 0.0 copy-done.1
  20.6 0.7 and_convert_fusion
  21.3 0.2 convert_reduce_fusion
  21.5 66.5 %all-to-all-done = f32[32,8,24,128]{3,1,2,0:T(8,128)S(1)} async-done(((f32[32,8,24,128]{3,1,2,0:T(8,128)}), f32[32,8,24,128]{3,1,2,0:T(8,128)S(1)}, u32[]{:S(2)}, u32[]{:S(2)}) %all-to-all-start) | async-done | bytes 3145760 | tf_op jit(solution)/shard_map/all_to_all | solution.py:44
  88.0 2.4 %copy.23 = f32[3072,256]{1,0:T(8,128)} copy(f32[3072,256]{0,1:T(8,128)S(1)} %bitcast.41) | data formatting | bytes 6291456 | tf_op jit(solution)/shard_map/dot_general | solution.py:14
  90.3 3.5 %convolution_multiply_fusion = f32[256,24,128]{0,2,1:T(8,128)S(1)} fusion(f32[24,128,256]{2,1,0:T(8,128)} %bitcast.42, f32[256]{0:T(256)S(1)} %get-tuple-element.7, s32[256]{0:T(256)S(1)} %multiply_add_fusion.1), kind=kOutput, calls=%fused_computation.3 | convolution fusion | flops 2416771072 | bytes 6293504 | tf_op jit(solution)/shard_map/dot_general | solution.py:14
  93.9 0.3 slice_reduce_fusion
  94.2 0.1 fusion.29
  94.3 1.9 %collective-permute-start.1 = (f32[24]{0:T(128)S(1)}, f32[24]{0:T(128)S(1)}, u32[]{:S(2)}, u32[]{:S(2)}) collective-permute-start(f32[24]{0:T(128)S(1)} %slice_reduce_fusion), channel_id=1, source_target_pairs={{1,0},{2,1},{3,2},{4,3},{5,4},{6,5},{7,6},{8,7},{9,8},{10,9},{11,1... | collective-permute-start | bytes 296 | tf_op jit(solution)/shard_map/ppermute | solution.py:10
  96.2 0.4 dynamic-slice_reduce_fusion
  96.6 3.4 %collective-permute-start = (f32[24]{0:T(128)S(1)}, f32[24]{0:T(128)S(1)}, u32[]{:S(2)}, u32[]{:S(2)}) collective-permute-start(f32[24]{0:T(128)S(1)} %dynamic-slice_reduce_fusion), channel_id=1, source_target_pairs={{0,1},{1,2},{2,3},{3,4},{4,5},{5,6},{6,7},{7,8},{8,9},{9,10},{10,1... | collective-permute-start | bytes 296 | tf_op jit(solution)/shard_map/ppermute | solution.py:10
  100.0 5.1 %collective-permute-done = f32[24]{0:T(128)S(1)} collective-permute-done((f32[24]{0:T(128)S(1)}, f32[24]{0:T(128)S(1)}, u32[]{:S(2)}, u32[]{:S(2)}) %collective-permute-start) | collective-permute-done | bytes 128 | tf_op jit(solution)/shard_map/ppermute | solution.py:10
  105.1 0.1 copy.26
  105.2 0.1 maximum_multiply_fusion
  105.3 0.0 collective-permute-done.1
  105.3 0.1 select_multiply_fusion
  105.3 5.1 %add_multiply_fusion = f32[256,24,128]{0,2,1:T(8,128)} fusion(f32[128]{0:T(128)S(1)} %get-tuple-element.9, f32[256,24]{0,1:T(8,128)S(1)} %select_multiply_fusion, f32[128]{0:T(128)S(1)} %get-tuple-element.10, f32[256,24]{0,1:T(8,128)S(1)} %maximum_multiply_fusion, f32[256]{0:T(256)S(1)} %get-tuple-element.7, f32[256,24,128]{0,2,1:T(8,128)S(1)} %convolution_multiply_fusion), kind=kOutput, calls=%fused_computation.1 | convolution fusion | flops 1211990016 | bytes 6342656 | tf_op jit(solution)/shard_map/dot_general | solution.py:72
  110.4 3.5 %copy.28 = f32[256,24,128]{2,1,0:T(8,128)} copy(f32[256,24,128]{0,2,1:T(8,128)} %add_multiply_fusion) | data formatting | bytes 6291456 | tf_op jit(solution)/shard_map/mul | solution.py:84
  (12 shorter events, 0.1 us)
Async XLA Ops:
  8.5 7.1 %copy-start.2 = (s32[32]{0:T(128)S(1)}, s32[32]{0:T(128)}, u32[]{:S(2)}) copy-start(s32[32]{0:T(128)} %param.8) | copy-start | bytes 388
  8.5 10.3 %copy-start = (s32[4096]{0:T(1024)S(1)}, s32[4096]{0:T(1024)}, u32[]{:S(2)}) copy-start(s32[4096]{0:T(1024)} %param.7) | copy-start | bytes 49156
  8.5 12.1 %copy-start.1 = (s32[256]{0:T(256)S(1)}, s32[256]{0:T(256)}, u32[]{:S(2)}) copy-start(s32[256]{0:T(256)} %param.9) | copy-start | bytes 3076
  8.5 79.5 %all-to-all-start = ((f32[32,8,24,128]{3,1,2,0:T(8,128)}), f32[32,8,24,128]{3,1,2,0:T(8,128)S(1)}, u32[]{:S(2)}, u32[]{:S(2)}) async-start(f32[32,8,24,128]{3,1,2,0:T(8,128)} %fusion.4), calls=%async_computation | async-start | bytes 6291456 | tf_op jit(solution)/shard_map/all_to_all | solution.py:44
  94.3 11.0 %collective-permute-start.1 = (f32[24]{0:T(128)S(1)}, f32[24]{0:T(128)S(1)}, u32[]{:S(2)}, u32[]{:S(2)}) collective-permute-start(f32[24]{0:T(128)S(1)} %slice_reduce_fusion), channel_id=1, source_target_pairs={{1,0},{2,1},{3,2},{4,3},{5,4},{6,5},{7,6},{8,7},{9,8},{10,9},{11,1... | collective-permute-start | bytes 296 | tf_op jit(solution)/shard_map/ppermute | solution.py:10
  96.6 8.5 %collective-permute-start = (f32[24]{0:T(128)S(1)}, f32[24]{0:T(128)S(1)}, u32[]{:S(2)}, u32[]{:S(2)}) collective-permute-start(f32[24]{0:T(128)S(1)} %dynamic-slice_reduce_fusion), channel_id=1, source_target_pairs={{0,1},{1,2},{2,3},{3,4},{4,5},{5,6},{6,7},{7,8},{8,9},{9,10},{10,1... | collective-permute-start | bytes 296 | tf_op jit(solution)/shard_map/ppermute | solution.py:10
where the time goes:
time: 114 us
  waiting for transfers between devices  71.6 us (63%)
  starting transfers between devices  12.4 us (11%)
  matrix products  11.7 us (10%)
  local copies, waits for them, and re-layouts  11.2 us (10%)
  other arithmetic  5.48 us (5%)
  between operations  1.59 us (1%)
    all_to_all x1, waiting for transfers between devices, on_device(): lax.all_to_all(sendbuf, ('grp', 'dev'), split_axis=0, concat_axis=0, tile...  66.5 us
    all_to_all x1, starting transfers between devices, on_device(): lax.all_to_all(sendbuf, ('grp', 'dev'), split_axis=0, concat_axis=0, tile...  7.08 us
    dot_general x2, matrix products, select_rows(): jnp.dot(picks, table, precision=lax.Precision.HIGHEST, preferred_element_...  6.65 us
    ppermute x2, starting transfers between devices, passed_along(): lax.ppermute(value, axis, [(source, source + steps) for source in range(i...  5.28 us
    ppermute x2, waiting for transfers between devices, passed_along(): lax.ppermute(value, axis, [(source, source + steps) for source in range(i...  5.09 us
    dot_general x1, matrix products, on_device(): jnp.dot(masked.reshape(capacity * fields, cells), stencil, precision=lax....  5.09 us
    mul x1, local copies, waits for them, and re-layouts, on_device(): smoothed = (inner + edges_added) * wet[:, None, None]  3.54 us
    dot_general x2, local copies, waits for them, and re-layouts, select_rows(): jnp.dot(picks, table, precision=lax.Precision.HIGHEST, preferred_element_...  2.81 us
  transfers between devices with their start and end apart: 3, of which 2 were waited for; matrix products, arithmetic and copies ran while one was open for 4% of the time, Pallas kernels for 0%

commit v1 on v0

v1 whole, which is shorter than its diff:
```python
import functools

import jax
import jax.numpy as jnp
from jax import lax
from jax.experimental import pallas as pl
from jax.experimental.pallas import tpu as pltpu
from jax.sharding import PartitionSpec as P

AXES = ("grp", "dev")
TILE = 8


def passed_along(value, axis, steps):
    count = lax.axis_size(axis)
    initial, last = (max(0, -steps), min(count, count - steps))
    return lax.ppermute(value, axis, [(source, source + steps) for source in range(initial, last)])


def pack_body(table, accum, counts, out, *, windows, owners, pair_most):
    _, fields, cells = accum.shape
    tiles = fields // TILE
    step = pl.program_id(0)
    per_step = out.shape[0]
    scale = jnp.broadcast_to(1.0 / counts[...].astype(jnp.float32), (fields, cells))
    lane = lax.broadcasted_iota(jnp.int32, (TILE, cells), 1)

    def block_at(window):
        local = table[jnp.clip(window, 0, windows - 1)]
        return accum[local] * scale

    for item in range(per_step):
        owner = step * per_step + item
        first = table[windows + owner]
        after = table[windows + owner + 1]
        for rank in range(pair_most):
            out[item, pl.ds(rank * fields, fields), :] = block_at(first + rank)
        left = block_at(first - 1)
        right = block_at(after)
        edge = jnp.zeros((TILE, cells), jnp.float32)
        for tile in range(tiles):
            rows = slice(tile * TILE, (tile + 1) * TILE)
            right_at = pltpu.roll(right[rows], tile, 1) if tile else right[rows]
            left_at = pltpu.roll(left[rows], cells - tile, 1) if tile else left[rows]
            edge = jnp.where(lane == tile, right_at, edge)
            edge = jnp.where(lane == cells - 1 - tile, left_at, edge)
        out[item, pl.ds(pair_most * fields, TILE), :] = edge


def pack(table, accum, counts, windows, owners, pair_most):
    blocks, fields, cells = accum.shape
    rows = pair_most * fields + TILE
    steps = 8
    per_step = owners // steps
    return pl.pallas_call(
        functools.partial(pack_body, windows=windows, owners=owners, pair_most=pair_most),
        out_shape=jax.ShapeDtypeStruct((owners, rows, cells), jnp.float32),
        grid_spec=pltpu.PrefetchScalarGridSpec(
            num_scalar_prefetch=1,
            grid=(steps,),
            in_specs=[
                pl.BlockSpec((blocks, fields, cells), lambda i, t: (0, 0, 0)),
                pl.BlockSpec((fields, 1), lambda i, t: (0, 0)),
            ],
            out_specs=pl.BlockSpec((per_step, rows, cells), lambda i, t: (i, 0, 0)),
        ),
        name="pack",
    )(table, accum, counts)


def place_body(info, received, out, *, capacity):
    chunk, fields, cells = out.shape
    tiles = fields // TILE
    base = pl.program_id(0) * chunk
    left_row = pl.multiple_of(info[2 * capacity], TILE)
    right_row = pl.multiple_of(info[2 * capacity + 1], TILE)
    left_wet = info[2 * capacity + 2].astype(jnp.float32)
    right_wet = info[2 * capacity + 3].astype(jnp.float32)
    last = info[2 * capacity + 4]
    left_tile = received[pl.ds(left_row, TILE), :] * left_wet
    right_tile = received[pl.ds(right_row, TILE), :] * right_wet
    left_edge = jnp.concatenate([pltpu.roll(left_tile, tile + 1, 1) for tile in range(tiles)], axis=0)
    right_edge = jnp.concatenate(
        [pltpu.roll(right_tile, cells - 1 - tile, 1) for tile in range(tiles)], axis=0
    )
    lane = lax.broadcasted_iota(jnp.int32, (fields, cells), 1)

    def masked_at(slot):
        row = pl.multiple_of(info[slot], TILE)
        wet = info[capacity + slot].astype(jnp.float32)
        return received[pl.ds(row, fields), :] * wet, wet

    before_block, _ = masked_at(jnp.maximum(base - 1, 0))
    before = jnp.where(base == 0, left_edge, pltpu.roll(before_block, 1, 1))
    block, wet = masked_at(base)
    ahead = pltpu.roll(block, cells - 1, 1)
    for item in range(chunk):
        slot = base + item
        after_slot = jnp.minimum(slot + 1, capacity - 1) if item == chunk - 1 else slot + 1
        after_block, after_wet = masked_at(after_slot)
        behind = pltpu.roll(block, 1, 1)
        after_ahead = pltpu.roll(after_block, cells - 1, 1)
        coming = jnp.where(slot == last, right_edge, after_ahead)
        sides = jnp.where(lane == 0, before, behind) + jnp.where(lane == cells - 1, coming, ahead)
        out[item] = (0.25 * sides + 0.5 * block) * wet
        before, block, wet, ahead = behind, after_block, after_wet, after_ahead


def place(info, received, capacity, fields, cells):
    steps = 8
    chunk = capacity // steps
    return pl.pallas_call(
        functools.partial(place_body, capacity=capacity),
        out_shape=jax.ShapeDtypeStruct((capacity, fields, cells), jnp.float32),
        grid_spec=pltpu.PrefetchScalarGridSpec(
            num_scalar_prefetch=1,
            grid=(steps,),
            in_specs=[pl.BlockSpec(received.shape, lambda i, t: (0, 0))],
            out_specs=pl.BlockSpec((chunk, fields, cells), lambda i, t: (i, 0, 0)),
        ),
        name="place",
    )(info, received)


def on_device(accum, step_count, stretch_slot, span_length, wet_mask):
    devices = lax.axis_size(AXES)
    me = lax.axis_index(AXES)
    blocks_dev, fields, cells = accum.shape
    capacity = wet_mask.shape[0]
    pair_most = capacity // devices
    all_blocks = stretch_slot.shape[0]
    windows = all_blocks // devices
    rows = pair_most * fields + TILE

    by_window = stretch_slot.reshape(windows, devices)
    here = by_window // blocks_dev == me
    ids = jnp.arange(all_blocks, dtype=jnp.int32).reshape(windows, devices)
    local = jnp.sum(jnp.where(here, by_window % blocks_dev, 0), axis=1)
    my_global = jnp.sum(jnp.where(here, ids, 0), axis=1)
    owner_ids = jnp.arange(devices, dtype=jnp.int32)
    edge_ids = jnp.arange(devices + 1, dtype=jnp.int32)
    starts = jnp.sum(jnp.where(owner_ids[None, :] < edge_ids[:, None], span_length[None, :], 0), axis=1)
    first_window = jnp.sum((my_global[None, :] < starts[:, None]).astype(jnp.int32), axis=1)
    table = jnp.concatenate([local, first_window])
    sendbuf = pack(table, accum, step_count.reshape(fields, 1), windows, devices, pair_most)
    received = lax.all_to_all(sendbuf, AXES, split_axis=0, concat_axis=0, tiled=True)
    received = received.reshape(devices * rows, cells)

    length = span_length[me]
    start = jnp.sum(jnp.where(owner_ids < me, span_length, 0))
    slots = jnp.arange(capacity, dtype=jnp.int32)
    valid = slots < length
    wet = jnp.where(valid & (wet_mask == 1), 1, 0)
    left_wet = passed_along(wet[length - 1], AXES, 1)
    right_wet = passed_along(wet[0], AXES, -1)
    padded = jnp.pad(stretch_slot, (1, capacity + 1))
    around = lax.dynamic_slice_in_dim(padded, start, capacity + 2) // blocks_dev
    sender = around[1:-1]
    opening = start // devices
    opening_senders = lax.dynamic_slice_in_dim(stretch_slot, opening * devices, devices) // blocks_dev
    skipped = (opening_senders[None, :] == sender[:, None]) & (owner_ids < start % devices)[None, :]
    rank = (start + slots) // devices - opening - jnp.sum(skipped.astype(jnp.int32), axis=1)
    row_of = jnp.where(valid, sender * rows + rank * fields, 0)
    edge_row = pair_most * fields
    left_row = around[0] * rows + edge_row
    right_row = jnp.sum(jnp.where(slots == length - 1, around[2:], 0)) * rows + edge_row
    ends = jnp.stack([left_row, right_row, left_wet, right_wet, length - 1])
    info = jnp.concatenate([row_of, wet, ends])
    return place(info, received, capacity, fields, cells)


def solution(mesh):
    return jax.shard_map(
        on_device,
        mesh=mesh,
        in_specs=(P(AXES, None, None), P(), P(), P(), P(AXES)),
        out_specs=P(AXES, None, None),
        check_vma=False,
    )
```

time: 114 us -> 103 us (0.904); the launches traced: 114 us -> 101 us
  waiting for transfers between devices: 71.6 us -> 52.7 us
  Pallas kernels: 0 us -> 13.2 us
  matrix products: 11.7 us -> 0 us
  between operations: 1.59 us -> 6.35 us
  starting transfers between devices: 12.4 us -> 16.2 us
  local copies, waits for them, and re-layouts: 11.2 us -> 7.47 us
    all_to_all x1, waiting for transfers between devices: 66.5 us -> 13.7 us  [on_device(): lax.all_to_all(sendbuf, AXES, split_axis=0, concat_axis=0, tiled=True)]
    ppermute x2, waiting for transfers between devices: 5.09 us -> 39 us  [passed_along(): lax.ppermute(value, axis, [(source, source + steps) for source in range(i...]
    pallas_call x0 -> x2, Pallas kernels: none -> 13.2 us  [the longest x1 7.08 us: place(): pl.pallas_call(functools.partial(place_body, capacity=capacity), out_shap...]
    dot_general x3 -> x0, matrix products: 11.7 us -> none  [the longest x2 6.65 us: select_rows(): jnp.dot(picks, table, precision=lax.Precision.HIGHEST, preferred_element_...]
    ppermute x2, starting transfers between devices: 5.28 us -> 9.15 us  [passed_along(): lax.ppermute(value, axis, [(source, source + steps) for source in range(i...]
    mul x1 -> x0, local copies, waits for them, and re-layouts: 3.54 us -> none  [on_device(): smoothed = (inner + edges_added) * wet[:, None, None]]
    dot_general x2 -> x0, local copies, waits for them, and re-layouts: 2.81 us -> none  [select_rows(): jnp.dot(picks, table, precision=lax.Precision.HIGHEST, preferred_element_...]
    reduce_sum x4 -> x6, other arithmetic: 1.6 us -> 3.73 us  [the longest x1 1.92 us: on_device(): jnp.sum(jnp.where(slots == length - 1, around[2:], 0)) * rows + edge_row]
  transfers between devices with their start and end apart: 3 -> 3, of which waited for: 2 -> 3; matrix products, arithmetic and copies ran while one was open for 4% -> 7% of each run, Pallas kernels for 0% -> 0%
where the time goes in v1:
time: 103 us; the launch traced here: 101 us
  waiting for transfers between devices  52.7 us (51%)
  starting transfers between devices  16.2 us (16%)
  Pallas kernels  13.2 us (13%)
  local copies, waits for them, and re-layouts  7.47 us (7%)
  between operations  6.35 us (6%)
  other arithmetic  5.02 us (5%)
    ppermute x2, waiting for transfers between devices, passed_along(): lax.ppermute(value, axis, [(source, source + steps) for source in range(i...  39 us
    all_to_all x1, waiting for transfers between devices, on_device(): lax.all_to_all(sendbuf, AXES, split_axis=0, concat_axis=0, tiled=True)  13.7 us
    ppermute x2, starting transfers between devices, passed_along(): lax.ppermute(value, axis, [(source, source + steps) for source in range(i...  9.15 us
    all_to_all x1, starting transfers between devices, on_device(): lax.all_to_all(sendbuf, AXES, split_axis=0, concat_axis=0, tiled=True)  7.09 us
    pallas_call x1, Pallas kernels, place(): pl.pallas_call(functools.partial(place_body, capacity=capacity), out_shap...  7.08 us
    pallas_call x1, Pallas kernels, pack(): pl.pallas_call(functools.partial(pack_body, windows=windows, owners=owner...  6.15 us
  transfers between devices with their start and end apart: 3, of which 3 were waited for; matrix products, arithmetic and copies ran while one was open for 7% of the time, Pallas kernels for 0%

profile of v1, /device:TPU:1, one launch (start us, length us, event | category | flops | bytes accessed | tf_op | source)
XLA Modules:
  0.0 101.0 jit_solution(12009104882054312874)
XLA Ops:
  0.0 0.7 select_reduce_fusion.1
  0.7 1.3 %copy.8.counts = s32[24,1]{1,0:T(8,128)} copy(s32[24,1]{0,1:T(1,128)} %bitcast.10) | data formatting | bytes 192 | tf_op jit(solution)/shard_map/reshape | solution.py:145
  2.1 0.8 reshape.30
  2.9 0.2 fusion.2
  3.0 0.2 convert_reduce_fusion.1
  3.2 0.6 pad_add_fusion.table
  3.8 6.2 %pack.1 = f32[32,200,128]{2,1,0:T(8,128)} custom-call(s32[161]{0:T(256)} %pad_add_fusion.table, f32[128,24,128]{2,1,0:T(8,128)} %accum.1, s32[24,1]{1,0:T(8,128)} %copy.8.counts), custom_call_target="tpu_custom_call" | custom-call | tf_op jit(solution)/shard_map/pack/pallas_call | solution.py:55
  9.9 0.0 copy-start.3
  9.9 0.0 copy-start.2
  9.9 0.0 copy-start.1
  9.9 7.1 %all-to-all-start = ((f32[32,200,128]{2,1,0:T(8,128)}), f32[32,200,128]{2,1,0:T(8,128)S(1)}, u32[]{:S(2)}, u32[]{:S(2)}) async-start(f32[32,200,128]{2,1,0:T(8,128)} %pack.1), calls=%async_computation | async-start | bytes 6553600 | tf_op jit(solution)/shard_map/all_to_all | solution.py:146
  17.0 0.0 copy-done.3
  17.0 0.6 dynamic_slice.12
  18.7 0.0 copy-done.2
  18.8 0.6 and_select_fusion
  19.3 0.6 fusion.9
  19.9 7.2 %collective-permute-start.1 = (s32[]{:T(128)}, s32[]{:T(128)}, u32[]{:S(2)}, u32[]{:S(2)}) collective-permute-start(s32[]{:T(128)} %bitcast.4), channel_id=1, source_target_pairs={{1,0},{2,1},{3,2},{4,3},{5,4},{6,5},{7,6},{8,7},{9,8},{10,9},{11,1... | collective-permute-start | bytes 20 | tf_op jit(solution)/shard_map/ppermute | solution.py:17
  27.2 1.9 %collective-permute-start = (s32[]{:T(128)}, s32[]{:T(128)}, u32[]{:S(2)}, u32[]{:S(2)}) collective-permute-start(s32[]{:T(128)} %bitcast.2), channel_id=1, source_target_pairs={{0,1},{1,2},{2,3},{3,4},{4,5},{5,6},{6,7},{7,8},{8,9},{9,10},{10,1... | collective-permute-start | bytes 20 | tf_op jit(solution)/shard_map/ppermute | solution.py:17
  29.1 0.6 fusion.8
  33.6 0.0 copy-done.1
  33.6 0.1 add_select_fusion.2
  33.7 0.5 slice.13
  34.3 0.1 slice.12
  35.0 0.1 and_select_fusion.1
  35.1 0.1 convert_reduce_fusion
  35.1 1.9 %fusion.7 = (s32[]{:T(128)}, s32[256]{0:T(256)S(1)}) fusion(s32[258]{0:T(512)S(1)} %add_select_fusion.2, s32[]{:T(128)} %sub.49, s32[256]{0:T(256)S(1)} %convert_reduce_fusion, s32[]{:T(128)S(6)} %select_n.80, s32[]{:T(128)} %fusion.8, s32[]{:T(128)} %bitcast), kind=kLoop, calls=%fused_computation.35 | loop fusion | flops 6655 | bytes 4116 | tf_op jit(solution)/shard_map/reduce_sum | solution.py:166
  37.7 36.1 %collective-permute-done.1 = s32[]{:T(128)} collective-permute-done((s32[]{:T(128)}, s32[]{:T(128)}, u32[]{:S(2)}, u32[]{:S(2)}) %collective-permute-start.1) | collective-permute-done | bytes 36 | tf_op jit(solution)/shard_map/ppermute | solution.py:17
  73.8 2.9 %collective-permute-done = s32[]{:T(128)} collective-permute-done((s32[]{:T(128)}, s32[]{:T(128)}, u32[]{:S(2)}, u32[]{:S(2)}) %collective-permute-start) | collective-permute-done | bytes 36 | tf_op jit(solution)/shard_map/ppermute | solution.py:17
  76.7 1.8 %concatenate.6.info = s32[517]{0:T(1024)} concatenate(s32[256]{0:T(256)S(1)} %get-tuple-element.8, s32[256]{0:T(256)S(1)} %and_select_fusion, s32[1]{0:T(128)S(6)} %add.60, s32[1]{0:T(128)} %bitcast.1, s32[1]{0:T(128)} %bitcast.3, s32[1]{0:T(128)} %bitcast.5, s32[1]{0:T(128)} %bitcast.6), dimensions={0} | concatenate | bytes 4136 | tf_op jit(solution)/shard_map/concatenate | solution.py:168
  78.6 13.7 %all-to-all-done = f32[32,200,128]{2,1,0:T(8,128)S(1)} async-done(((f32[32,200,128]{2,1,0:T(8,128)}), f32[32,200,128]{2,1,0:T(8,128)S(1)}, u32[]{:S(2)}, u32[]{:S(2)}) %all-to-all-start) | async-done | bytes 3276832 | tf_op jit(solution)/shard_map/all_to_all | solution.py:146
  92.2 0.0 copy-start
  92.2 1.7 %copy-done = f32[32,200,128]{2,1,0:T(8,128)} copy-done((f32[32,200,128]{2,1,0:T(8,128)}, f32[32,200,128]{2,1,0:T(8,128)S(1)}, u32[]{:S(2)}) %copy-start) | copy-done | bytes 3276824
  93.9 7.1 %place.1 = f32[256,24,128]{2,1,0:T(8,128)} custom-call(s32[517]{0:T(1024)} %concatenate.6.info, f32[6400,128]{1,0:T(8,128)} %bitcast.9), custom_call_target="tpu_custom_call" | custom-call | tf_op jit(solution)/shard_map/place/pallas_call | solution.py:112
  (1 shorter events, 0.0 us)
Async XLA Ops:
  9.9 7.1 %copy-start.3 = (s32[32]{0:T(128)S(1)}, s32[32]{0:T(128)}, u32[]{:S(2)}) copy-start(s32[32]{0:T(128)} %param.8) | copy-start | bytes 388
  9.9 8.8 %copy-start.2 = (s32[256]{0:T(256)S(1)}, s32[256]{0:T(256)}, u32[]{:S(2)}) copy-start(s32[256]{0:T(256)} %param.9) | copy-start | bytes 3076
  9.9 23.7 %copy-start.1 = (s32[4096]{0:T(1024)S(1)}, s32[4096]{0:T(1024)}, u32[]{:S(2)}) copy-start(s32[4096]{0:T(1024)} %param.7) | copy-start | bytes 49156
  9.9 82.3 %all-to-all-start = ((f32[32,200,128]{2,1,0:T(8,128)}), f32[32,200,128]{2,1,0:T(8,128)S(1)}, u32[]{:S(2)}, u32[]{:S(2)}) async-start(f32[32,200,128]{2,1,0:T(8,128)} %pack.1), calls=%async_computation | async-start | bytes 6553600 | tf_op jit(solution)/shard_map/all_to_all | solution.py:146
  19.9 53.9 %collective-permute-start.1 = (s32[]{:T(128)}, s32[]{:T(128)}, u32[]{:S(2)}, u32[]{:S(2)}) collective-permute-start(s32[]{:T(128)} %bitcast.4), channel_id=1, source_target_pairs={{1,0},{2,1},{3,2},{4,3},{5,4},{6,5},{7,6},{8,7},{9,8},{10,9},{11,1... | collective-permute-start | bytes 20 | tf_op jit(solution)/shard_map/ppermute | solution.py:17
  27.2 49.5 %collective-permute-start = (s32[]{:T(128)}, s32[]{:T(128)}, u32[]{:S(2)}, u32[]{:S(2)}) collective-permute-start(s32[]{:T(128)} %bitcast.2), channel_id=1, source_target_pairs={{0,1},{1,2},{2,3},{3,4},{4,5},{5,6},{6,7},{7,8},{8,9},{9,10},{10,1... | collective-permute-start | bytes 20 | tf_op jit(solution)/shard_map/ppermute | solution.py:17
  92.2 1.7 %copy-start = (f32[32,200,128]{2,1,0:T(8,128)}, f32[32,200,128]{2,1,0:T(8,128)S(1)}, u32[]{:S(2)}) copy-start(f32[32,200,128]{2,1,0:T(8,128)S(1)} %all-to-all-done) | copy-start | bytes 9830404

commit v2 on v1

v2 whole, which is shorter than its diff:
```python
import functools

import jax
import jax.numpy as jnp
from jax import lax
from jax.experimental import pallas as pl
from jax.experimental.pallas import tpu as pltpu
from jax.sharding import PartitionSpec as P

AXES = ("grp", "dev")
TILE = 8


def passed_along(value, axis, steps):
    count = lax.axis_size(axis)
    initial, last = (max(0, -steps), min(count, count - steps))
    return lax.ppermute(value, axis, [(source, source + steps) for source in range(initial, last)])


def pack_body(table, accum, out, *, windows, pair_most):
    fields = accum.shape[1]

    def one_owner(owner, carry):
        first = table[windows + owner]
        for rank in range(pair_most):
            local = table[jnp.minimum(first + rank, windows - 1)]
            out[owner, pl.ds(rank * fields, fields), :] = accum[local]
        return carry

    lax.fori_loop(0, out.shape[0], one_owner, 0, unroll=2)


def pack(table, accum, windows, owners, pair_most):
    blocks, fields, cells = accum.shape
    return pl.pallas_call(
        functools.partial(pack_body, windows=windows, pair_most=pair_most),
        out_shape=jax.ShapeDtypeStruct((owners, pair_most * fields, cells), jnp.float32),
        in_specs=[
            pl.BlockSpec(memory_space=pltpu.SMEM),
            pl.BlockSpec(memory_space=pltpu.VMEM),
        ],
        out_specs=pl.BlockSpec(memory_space=pltpu.VMEM),
        name="pack",
    )(table, accum)


def edges_body(table, held, accum, out, *, windows, owners):
    _, fields, cells = accum.shape
    tiles = fields // TILE
    group = cells // tiles
    half = out.shape[0] // 2
    lane = lax.broadcasted_iota(jnp.int32, (TILE, cells), 1)
    out[...] = jnp.zeros(out.shape, jnp.float32)

    def one_owner(owner, carry):
        first = table[windows + owner]
        after = table[windows + owner + 1]
        row = pl.multiple_of(owner // group * TILE, TILE)
        at = owner % group * tiles
        sides = (
            (0, first - 1, held[owner], cells - 1),
            (half, after, held[owners + 1 + owner + 1], 0),
        )
        for base, window, has, cell in sides:
            block = accum[table[jnp.clip(window, 0, windows - 1)]]
            for tile in range(tiles):
                turned = pltpu.roll(block[tile * TILE:(tile + 1) * TILE], (at + tile + cells - cell) % cells, 1)
                kept = (lane == at + tile) & (has > 0)
                rows = pl.ds(pl.multiple_of(base + row, TILE), TILE)
                out[rows, :] = jnp.where(kept, turned, out[rows, :])
        return carry

    lax.fori_loop(0, owners, one_owner, 0)


def edges(table, held, accum, windows, owners):
    _, fields, cells = accum.shape
    group = cells // (fields // TILE)
    height = 2 * TILE * pl.cdiv(owners, group)
    return pl.pallas_call(
        functools.partial(edges_body, windows=windows, owners=owners),
        out_shape=jax.ShapeDtypeStruct((height, cells), jnp.float32),
        in_specs=[
            pl.BlockSpec(memory_space=pltpu.SMEM),
            pl.BlockSpec(memory_space=pltpu.SMEM),
            pl.BlockSpec(memory_space=pltpu.VMEM),
        ],
        out_specs=pl.BlockSpec(memory_space=pltpu.VMEM),
        name="edges",
    )(table, held, accum)


def place_body(info, received, ends, counts, out, *, capacity):
    chunk, fields, cells = out.shape
    tiles = fields // TILE
    base = pl.program_id(0) * chunk
    half = ends.shape[0] // 2
    left_wet = info[2 * capacity].astype(jnp.float32)
    right_wet = info[2 * capacity + 1].astype(jnp.float32)
    last = info[2 * capacity + 2]
    end_row = pl.multiple_of(info[2 * capacity + 3], TILE)
    end_lane = info[2 * capacity + 4]
    left_tile = ends[pl.ds(end_row, TILE), :] * left_wet
    right_tile = ends[pl.ds(pl.multiple_of(half + end_row, TILE), TILE), :] * right_wet
    left_edge = jnp.concatenate(
        [pltpu.roll(left_tile, (cells - end_lane - tile) % cells, 1) for tile in range(tiles)], axis=0
    )
    right_edge = jnp.concatenate(
        [pltpu.roll(right_tile, cells - 1 - end_lane - tile, 1) for tile in range(tiles)], axis=0
    )
    lane = lax.broadcasted_iota(jnp.int32, (fields, cells), 1)
    half_scale = jnp.broadcast_to(0.5 / counts[...].astype(jnp.float32), (fields, cells))

    def masked_at(slot):
        row = pl.multiple_of(info[slot], TILE)
        wet = info[capacity + slot].astype(jnp.float32)
        return received[pl.ds(row, fields), :] * wet, wet

    before_block, _ = masked_at(jnp.maximum(base - 1, 0))
    before = jnp.where(base == 0, left_edge, pltpu.roll(before_block, 1, 1))
    block, wet = masked_at(base)
    ahead = pltpu.roll(block, cells - 1, 1)
    for item in range(chunk):
        slot = base + item
        after_slot = jnp.minimum(slot + 1, capacity - 1) if item == chunk - 1 else slot + 1
        after_block, after_wet = masked_at(after_slot)
        behind = pltpu.roll(block, 1, 1)
        after_ahead = pltpu.roll(after_block, cells - 1, 1)
        coming = jnp.where(slot == last, right_edge, after_ahead)
        sides = jnp.where(lane == 0, before, behind) + jnp.where(lane == cells - 1, coming, ahead)
        out[item] = (0.5 * sides + block) * (half_scale * wet)
        before, block, wet, ahead = behind, after_block, after_wet, after_ahead


def place(info, received, ends, counts, capacity, fields, cells):
    steps = 8
    chunk = capacity // steps
    whole = pl.BlockSpec(memory_space=pltpu.VMEM)
    return pl.pallas_call(
        functools.partial(place_body, capacity=capacity),
        out_shape=jax.ShapeDtypeStruct((capacity, fields, cells), jnp.float32),
        grid=(steps,),
        in_specs=[pl.BlockSpec(memory_space=pltpu.SMEM), whole, whole, whole],
        out_specs=pl.BlockSpec((chunk, fields, cells), lambda i: (i, 0, 0)),
        name="place",
    )(info, received, ends, counts)


def on_device(accum, step_count, stretch_slot, span_length, wet_mask):
    devices = lax.axis_size(AXES)
    me = lax.axis_index(AXES)
    blocks_dev, fields, cells = accum.shape
    capacity = wet_mask.shape[0]
    pair_most = capacity // devices
    all_blocks = stretch_slot.shape[0]
    windows = all_blocks // devices
    rows = pair_most * fields

    by_window = stretch_slot.reshape(windows, devices)
    here = by_window // blocks_dev == me
    ids = jnp.arange(all_blocks, dtype=jnp.int32).reshape(windows, devices)
    local = jnp.sum(jnp.where(here, by_window % blocks_dev, 0), axis=1)
    my_global = jnp.sum(jnp.where(here, ids, 0), axis=1)
    owner_ids = jnp.arange(devices, dtype=jnp.int32)
    edge_ids = jnp.arange(devices + 1, dtype=jnp.int32)
    starts = jnp.sum(jnp.where(owner_ids[None, :] < edge_ids[:, None], span_length[None, :], 0), axis=1)
    first_window = jnp.sum((my_global[None, :] < starts[:, None]).astype(jnp.int32), axis=1)
    table = jnp.concatenate([local, first_window])
    sendbuf = pack(table, accum, windows, devices, pair_most)
    received = lax.all_to_all(sendbuf, AXES, split_axis=0, concat_axis=0, tiled=True)
    received = received.reshape(devices * rows, cells)

    offsets = jnp.concatenate([starts - 1, starts])
    held = jnp.sum((my_global[None, :] == offsets[:, None]).astype(jnp.int32), axis=1)
    ends = lax.psum(edges(table, held, accum, windows, devices), AXES)

    length = span_length[me]
    start = jnp.sum(jnp.where(owner_ids < me, span_length, 0))
    slots = jnp.arange(capacity, dtype=jnp.int32)
    valid = slots < length
    wet = jnp.where(valid & (wet_mask == 1), 1, 0)
    left_wet = passed_along(wet[length - 1], AXES, 1)
    right_wet = passed_along(wet[0], AXES, -1)
    padded = jnp.pad(stretch_slot, (0, capacity))
    sender = lax.dynamic_slice_in_dim(padded, start, capacity) // blocks_dev
    opening = start // devices
    opening_senders = lax.dynamic_slice_in_dim(stretch_slot, opening * devices, devices) // blocks_dev
    skipped = (opening_senders[None, :] == sender[:, None]) & (owner_ids < start % devices)[None, :]
    rank = (start + slots) // devices - opening - jnp.sum(skipped.astype(jnp.int32), axis=1)
    row_of = jnp.where(valid, sender * rows + rank * fields, 0)
    tiles = fields // TILE
    group = cells // tiles
    facts = jnp.stack([left_wet, right_wet, length - 1, me // group * TILE, me % group * tiles])
    info = jnp.concatenate([row_of, wet, facts])
    return place(info, received, ends, step_count.reshape(fields, 1), capacity, fields, cells)


def solution(mesh):
    return jax.shard_map(
        on_device,
        mesh=mesh,
        in_specs=(P(AXES, None, None), P(), P(), P(), P(AXES)),
        out_specs=P(AXES, None, None),
        check_vma=False,
    )
```

time: 103 us -> 117 us (1.14)
  blocking collectives: 0 us -> 68 us
  waiting for transfers between devices: 52.7 us -> 0.01 us
  Pallas kernels: 13.2 us -> 15 us
  between operations: 6.35 us -> 4.72 us
  local copies, waits for them, and re-layouts: 7.47 us -> 6.28 us
    psum x0 -> x1, blocking collectives: none -> 68 us  [on_device(): ends = lax.psum(edges(table, held, accum, windows, devices), AXES)]
    ppermute x2, waiting for transfers between devices: 39 us -> 0.01 us  [passed_along(): lax.ppermute(value, axis, [(source, source + steps) for source in range(i...]
    all_to_all x1, waiting for transfers between devices: 13.7 us -> 0.01 us  [on_device(): lax.all_to_all(sendbuf, AXES, split_axis=0, concat_axis=0, tiled=True)]
    pallas_call x1 -> x2, Pallas kernels: 6.15 us -> 8.54 us  [the longest x1 4.9 us: edges(): pl.pallas_call(functools.partial(edges_body, windows=windows, owners=owne...]
    select_n x1 -> x2, other arithmetic: 0.09 us -> 1.34 us  [the longest x1 1.25 us: on_device(): row_of = jnp.where(valid, sender * rows + rank * fields, 0)]
  transfers between devices with their start and end apart: 3 -> 3, of which waited for: 3 -> 0; matrix products, arithmetic and copies ran while one was open for 7% -> 6% of each run, Pallas kernels for 0% -> 4%
where the time goes in v2:
time: 117 us; the launch traced here: 116 us
  blocking collectives  68 us (58%)
  starting transfers between devices  16.2 us (14%)
  Pallas kernels  15 us (13%)
  local copies, waits for them, and re-layouts  6.28 us (5%)
  other arithmetic  5.3 us (5%)
  between operations  4.72 us (4%)
    psum x1, blocking collectives, on_device(): ends = lax.psum(edges(table, held, accum, windows, devices), AXES)  68 us
    ppermute x2, starting transfers between devices, passed_along(): lax.ppermute(value, axis, [(source, source + steps) for source in range(i...  9.15 us
    all_to_all x1, starting transfers between devices, on_device(): lax.all_to_all(sendbuf, AXES, split_axis=0, concat_axis=0, tiled=True)  7.09 us
    pallas_call x1, Pallas kernels, place(): pl.pallas_call(functools.partial(place_body, capacity=capacity), out_shap...  6.46 us
    pallas_call x1, Pallas kernels, edges(): pl.pallas_call(functools.partial(edges_body, windows=windows, owners=owne...  4.9 us
    pallas_call x1, Pallas kernels, pack(): pl.pallas_call(functools.partial(pack_body, windows=windows, pair_most=pa...  3.64 us
  transfers between devices with their start and end apart: 3, of which 0 were waited for; matrix products, arithmetic and copies ran while one was open for 6% of the time, Pallas kernels for 4%

profile of v2, /device:TPU:1, one launch (start us, length us, event | category | flops | bytes accessed | tf_op | source)
XLA Modules:
  0.0 115.6 jit_solution(12960470053018742653)
XLA Ops:
  0.0 0.8 reshape.26
  0.8 0.8 select_reduce_fusion.1
  1.5 0.2 fusion.2
  1.7 0.2 convert_reduce_fusion.2
  1.9 0.6 pad_add_fusion.table
  2.5 3.6 %pack.1 = f32[32,192,128]{2,1,0:T(8,128)} custom-call(s32[161]{0:T(256)} %pad_add_fusion.table, f32[128,24,128]{2,1,0:T(8,128)} %accum.3), custom_call_target="tpu_custom_call" | custom-call | tf_op jit(solution)/shard_map/pack/pallas_call | solution.py:35
  6.1 0.0 copy-start.4
  6.1 0.0 copy-start.2
  6.1 0.0 copy-start.3
  6.1 0.0 copy-start.1
  6.1 7.1 %all-to-all-start = ((f32[32,192,128]{2,1,0:T(8,128)}), f32[32,192,128]{2,1,0:T(8,128)S(1)}, u32[]{:S(2)}, u32[]{:S(2)}) async-start(f32[32,192,128]{2,1,0:T(8,128)} %pack.1), calls=%async_computation | async-start | bytes 6291456 | tf_op jit(solution)/shard_map/all_to_all | solution.py:170
  13.2 0.0 copy-done.4
  13.3 0.6 dynamic_slice.12
  15.1 0.0 copy-done.2
  15.1 0.6 and_select_fusion
  15.7 0.6 fusion.6
  16.3 3.2 %collective-permute-start = (s32[]{:T(128)}, s32[]{:T(128)}, u32[]{:S(2)}, u32[]{:S(2)}) collective-permute-start(s32[]{:T(128)} %bitcast.1), channel_id=1, source_target_pairs={{0,1},{1,2},{2,3},{3,4},{4,5},{5,6},{6,7},{7,8},{8,9},{9,10},{10,1... | collective-permute-start | bytes 20 | tf_op jit(solution)/shard_map/ppermute | solution.py:17
  19.6 5.9 %collective-permute-start.1 = (s32[]{:T(128)}, s32[]{:T(128)}, u32[]{:S(2)}, u32[]{:S(2)}) collective-permute-start(s32[]{:T(128)} %bitcast.3), channel_id=1, source_target_pairs={{1,0},{2,1},{3,2},{4,3},{5,4},{6,5},{7,6},{8,7},{9,8},{10,9},{11,1... | collective-permute-start | bytes 20 | tf_op jit(solution)/shard_map/ppermute | solution.py:17
  25.5 0.6 fusion.5
  29.5 0.1 pad_add_fusion.1
  29.6 0.8 convert_reduce_fusion.held
  30.4 4.9 %edges.1 = f32[16,128]{1,0:T(8,128)} custom-call(s32[161]{0:T(256)} %pad_add_fusion.table, s32[66]{0:T(128)} %convert_reduce_fusion.held, f32[128,24,128]{2,1,0:T(8,128)} %accum.3), custom_call_target="tpu_custom_call" | custom-call | tf_op jit(solution)/shard_map/edges/pallas_call | solution.py:80
  35.3 0.0 copy-done.3
  35.3 0.7 copy.8.counts
  36.0 68.0 %psum.7.ends = f32[16,128]{1,0:T(8,128)} all-reduce(f32[16,128]{1,0:T(8,128)} %edges.1), channel_id=1, replica_groups=mesh['grp'=2,'dev'=16] {'grp','dev'}, use_global_device_ids=true, to_apply=%region_7.8 | all-reduce | flops 2048 | bytes 16384 | tf_op jit(solution)/shard_map/psum | solution.py:175
  104.0 0.0 copy-done.1
  104.0 0.1 and_select_fusion.1
  104.1 0.1 and_select_fusion.3
  104.2 0.1 convert_reduce_fusion.1
  104.3 1.3 %add_select_fusion.2 = s32[256]{0:T(256)S(1)} fusion(s32[256]{0:T(256)S(1)} %convert_reduce_fusion.1, s32[]{:T(128)S(6)} %select_n.82, s32[]{:T(128)} %fusion.5, s32[]{:T(128)} %bitcast, s32[]{:T(128)S(6)} %select_n.79, s32[4096]{0:T(1024)S(1)} %copy-done.1), kind=kLoop, calls=%fused_computation.33 | loop fusion | flops 9728 | bytes 18448 | tf_op jit(solution)/shard_map/jit(_where)/select_n | solution.py:190
  105.5 0.0 collective-permute-done
  105.5 0.0 collective-permute-done.1
  105.5 1.9 %concatenate.9.info = s32[517]{0:T(1024)} concatenate(s32[256]{0:T(256)S(1)} %add_select_fusion.2, s32[256]{0:T(256)S(1)} %and_select_fusion, s32[1]{0:T(128)} %bitcast.2, s32[1]{0:T(128)} %bitcast.4, s32[1]{0:T(128)} %bitcast.5, s32[1]{0:T(128)} %bitcast.6, s32[1]{0:T(128)} %bitcast.7), dimensions={0} | concatenate | bytes 4136 | tf_op jit(solution)/shard_map/concatenate | solution.py:194
  107.5 0.0 all-to-all-done
  107.5 0.0 copy-start
  107.5 1.7 %copy-done = f32[32,192,128]{2,1,0:T(8,128)} copy-done((f32[32,192,128]{2,1,0:T(8,128)}, f32[32,192,128]{2,1,0:T(8,128)S(1)}, u32[]{:S(2)}) %copy-start) | copy-done | bytes 3145752
  109.1 6.5 %place.1 = f32[256,24,128]{2,1,0:T(8,128)} custom-call(s32[517]{0:T(1024)} %concatenate.9.info, f32[6144,128]{1,0:T(8,128)} %bitcast.10, f32[16,128]{1,0:T(8,128)} %psum.7.ends, s32[24,1]{1,0:T(8,128)} %copy.8.counts), custom_call_target="tpu_custom_call" | custom-call | tf_op jit(solution)/shard_map/place/pallas_call | solution.py:139
  (2 shorter events, 0.0 us)
Async XLA Ops:
  6.1 7.1 %copy-start.4 = (s32[32]{0:T(128)S(1)}, s32[32]{0:T(128)}, u32[]{:S(2)}) copy-start(s32[32]{0:T(128)} %param.8) | copy-start | bytes 388
  6.1 9.0 %copy-start.2 = (s32[256]{0:T(256)S(1)}, s32[256]{0:T(256)}, u32[]{:S(2)}) copy-start(s32[256]{0:T(256)} %param.9) | copy-start | bytes 3076
  6.1 29.1 %copy-start.3 = (s32[24]{0:T(128)S(1)}, s32[24]{0:T(128)}, u32[]{:S(2)}) copy-start(s32[24]{0:T(128)} %param.6) | copy-start | bytes 292
  6.1 97.9 %copy-start.1 = (s32[4096]{0:T(1024)S(1)}, s32[4096]{0:T(1024)}, u32[]{:S(2)}) copy-start(s32[4096]{0:T(1024)} %param.7) | copy-start | bytes 49156
  6.1 101.3 %all-to-all-start = ((f32[32,192,128]{2,1,0:T(8,128)}), f32[32,192,128]{2,1,0:T(8,128)S(1)}, u32[]{:S(2)}, u32[]{:S(2)}) async-start(f32[32,192,128]{2,1,0:T(8,128)} %pack.1), calls=%async_computation | async-start | bytes 6291456 | tf_op jit(solution)/shard_map/all_to_all | solution.py:170
  16.3 89.2 %collective-permute-start = (s32[]{:T(128)}, s32[]{:T(128)}, u32[]{:S(2)}, u32[]{:S(2)}) collective-permute-start(s32[]{:T(128)} %bitcast.1), channel_id=1, source_target_pairs={{0,1},{1,2},{2,3},{3,4},{4,5},{5,6},{6,7},{7,8},{8,9},{9,10},{10,1... | collective-permute-start | bytes 20 | tf_op jit(solution)/shard_map/ppermute | solution.py:17
  19.6 86.0 %collective-permute-start.1 = (s32[]{:T(128)}, s32[]{:T(128)}, u32[]{:S(2)}, u32[]{:S(2)}) collective-permute-start(s32[]{:T(128)} %bitcast.3), channel_id=1, source_target_pairs={{1,0},{2,1},{3,2},{4,3},{5,4},{6,5},{7,6},{8,7},{9,8},{10,9},{11,1... | collective-permute-start | bytes 20 | tf_op jit(solution)/shard_map/ppermute | solution.py:17
  107.5 1.7 %copy-start = (f32[32,192,128]{2,1,0:T(8,128)}, f32[32,192,128]{2,1,0:T(8,128)S(1)}, u32[]{:S(2)}) copy-start(f32[32,192,128]{2,1,0:T(8,128)S(1)} %all-to-all-done) | copy-start | bytes 9437188

commit v3 on v1

--- a/solution.py
+++ b/solution.py
@@ -9,6 +9,7 @@
 
 AXES = ("grp", "dev")
 TILE = 8
+SCRATCH_BYTES = 8 * 1024 * 1024
 
 
 def passed_along(value, axis, steps):
@@ -17,26 +18,25 @@
     return lax.ppermute(value, axis, [(source, source + steps) for source in range(initial, last)])
 
 
-def pack_body(table, accum, counts, out, *, windows, owners, pair_most):
+def in_vmem(value):
+    return pltpu.with_memory_space_constraint(value, pltpu.VMEM)
+
+
+def pack_body(table, accum, out, *, windows, pair_most):
     _, fields, cells = accum.shape
     tiles = fields // TILE
-    step = pl.program_id(0)
-    per_step = out.shape[0]
-    scale = jnp.broadcast_to(1.0 / counts[...].astype(jnp.float32), (fields, cells))
     lane = lax.broadcasted_iota(jnp.int32, (TILE, cells), 1)
 
     def block_at(window):
-        local = table[jnp.clip(window, 0, windows - 1)]
-        return accum[local] * scale
+        return accum[table[jnp.clip(window, 0, windows - 1)]]
 
-    for item in range(per_step):
-        owner = step * per_step + item
+    def one_owner(item, carry):
+        owner = pl.program_id(0) * out.shape[0] + item
         first = table[windows + owner]
-        after = table[windows + owner + 1]
         for rank in range(pair_most):
             out[item, pl.ds(rank * fields, fields), :] = block_at(first + rank)
         left = block_at(first - 1)
-        right = block_at(after)
+        right = block_at(table[windows + owner + 1])
         edge = jnp.zeros((TILE, cells), jnp.float32)
         for tile in range(tiles):
             rows = slice(tile * TILE, (tile + 1) * TILE)
@@ -45,38 +45,38 @@
             edge = jnp.where(lane == tile, right_at, edge)
             edge = jnp.where(lane == cells - 1 - tile, left_at, edge)
         out[item, pl.ds(pair_most * fields, TILE), :] = edge
+        return carry
+
+    lax.fori_loop(0, out.shape[0], one_owner, 0, unroll=4)
 
 
-def pack(table, accum, counts, windows, owners, pair_most):
+def pack(table, accum, windows, owners, pair_most):
     blocks, fields, cells = accum.shape
     rows = pair_most * fields + TILE
     steps = 8
-    per_step = owners // steps
     return pl.pallas_call(
-        functools.partial(pack_body, windows=windows, owners=owners, pair_most=pair_most),
+        functools.partial(pack_body, windows=windows, pair_most=pair_most),
         out_shape=jax.ShapeDtypeStruct((owners, rows, cells), jnp.float32),
-        grid_spec=pltpu.PrefetchScalarGridSpec(
-            num_scalar_prefetch=1,
-            grid=(steps,),
-            in_specs=[
-                pl.BlockSpec((blocks, fields, cells), lambda i, t: (0, 0, 0)),
-                pl.BlockSpec((fields, 1), lambda i, t: (0, 0)),
-            ],
-            out_specs=pl.BlockSpec((per_step, rows, cells), lambda i, t: (i, 0, 0)),
-        ),
+        grid=(steps,),
+        in_specs=[
+            pl.BlockSpec(memory_space=pltpu.SMEM),
+            pl.BlockSpec(memory_space=pltpu.VMEM),
+        ],
+        out_specs=pl.BlockSpec((owners // steps, rows, cells), lambda i: (i, 0, 0)),
+        compiler_params=pltpu.CompilerParams(vmem_limit_bytes=SCRATCH_BYTES),
         name="pack",
-    )(table, accum, counts)
+    )(table, in_vmem(accum))
 
 
-def place_body(info, received, out, *, capacity):
+def place_body(info, received, counts, out, *, capacity):
     chunk, fields, cells = out.shape
     tiles = fields // TILE
     base = pl.program_id(0) * chunk
-    left_row = pl.multiple_of(info[2 * capacity], TILE)
-    right_row = pl.multiple_of(info[2 * capacity + 1], TILE)
-    left_wet = info[2 * capacity + 2].astype(jnp.float32)
-    right_wet = info[2 * capacity + 3].astype(jnp.float32)
-    last = info[2 * capacity + 4]
+    left_wet = info[2 * capacity].astype(jnp.float32)
+    right_wet = info[2 * capacity + 1].astype(jnp.float32)
+    last = info[2 * capacity + 2]
+    left_row = pl.multiple_of(info[2 * capacity + 3], TILE)
+    right_row = pl.multiple_of(info[2 * capacity + 4], TILE)
     left_tile = received[pl.ds(left_row, TILE), :] * left_wet
     right_tile = received[pl.ds(right_row, TILE), :] * right_wet
     left_edge = jnp.concatenate([pltpu.roll(left_tile, tile + 1, 1) for tile in range(tiles)], axis=0)
@@ -84,6 +84,7 @@
         [pltpu.roll(right_tile, cells - 1 - tile, 1) for tile in range(tiles)], axis=0
     )
     lane = lax.broadcasted_iota(jnp.int32, (fields, cells), 1)
+    half_scale = jnp.broadcast_to(0.5 / counts[...].astype(jnp.float32), (fields, cells))
 
     def masked_at(slot):
         row = pl.multiple_of(info[slot], TILE)
@@ -102,24 +103,23 @@
         after_ahead = pltpu.roll(after_block, cells - 1, 1)
         coming = jnp.where(slot == last, right_edge, after_ahead)
         sides = jnp.where(lane == 0, before, behind) + jnp.where(lane == cells - 1, coming, ahead)
-        out[item] = (0.25 * sides + 0.5 * block) * wet
+        out[item] = (0.5 * sides + block) * (half_scale * wet)
         before, block, wet, ahead = behind, after_block, after_wet, after_ahead
 
 
-def place(info, received, capacity, fields, cells):
+def place(info, received, counts, capacity, fields, cells):
     steps = 8
     chunk = capacity // steps
+    whole = pl.BlockSpec(memory_space=pltpu.VMEM)
     return pl.pallas_call(
         functools.partial(place_body, capacity=capacity),
         out_shape=jax.ShapeDtypeStruct((capacity, fields, cells), jnp.float32),
-        grid_spec=pltpu.PrefetchScalarGridSpec(
-            num_scalar_prefetch=1,
-            grid=(steps,),
-            in_specs=[pl.BlockSpec(received.shape, lambda i, t: (0, 0))],
-            out_specs=pl.BlockSpec((chunk, fields, cells), lambda i, t: (i, 0, 0)),
-        ),
+        grid=(steps,),
+        in_specs=[pl.BlockSpec(memory_space=pltpu.SMEM), whole, whole],
+        out_specs=pl.BlockSpec((chunk, fields, cells), lambda i: (i, 0, 0)),
+        compiler_params=pltpu.CompilerParams(vmem_limit_bytes=SCRATCH_BYTES),
         name="place",
-    )(info, received)
+    )(info, in_vmem(received), in_vmem(counts))
 
 
 def on_device(accum, step_count, stretch_slot, span_length, wet_mask):
@@ -142,7 +142,7 @@
     starts = jnp.sum(jnp.where(owner_ids[None, :] < edge_ids[:, None], span_length[None, :], 0), axis=1)
     first_window = jnp.sum((my_global[None, :] < starts[:, None]).astype(jnp.int32), axis=1)
     table = jnp.concatenate([local, first_window])
-    sendbuf = pack(table, accum, step_count.reshape(fields, 1), windows, devices, pair_most)
+    sendbuf = pack(table, accum, windows, devices, pair_most)
     received = lax.all_to_all(sendbuf, AXES, split_axis=0, concat_axis=0, tiled=True)
     received = received.reshape(devices * rows, cells)
 
@@ -164,9 +164,9 @@
     edge_row = pair_most * fields
     left_row = around[0] * rows + edge_row
     right_row = jnp.sum(jnp.where(slots == length - 1, around[2:], 0)) * rows + edge_row
-    ends = jnp.stack([left_row, right_row, left_wet, right_wet, length - 1])
-    info = jnp.concatenate([row_of, wet, ends])
-    return place(info, received, capacity, fields, cells)
+    facts = jnp.stack([left_wet, right_wet, length - 1, left_row, right_row])
+    info = jnp.concatenate([row_of, wet, facts])
+    return place(info, received, step_count.reshape(fields, 1), capacity, fields, cells)
 
 
 def solution(mesh):

time: 103 us -> 95.8 us (0.930)
  Pallas kernels: 13.2 us -> 7.04 us
    pallas_call x1, Pallas kernels: 6.15 us -> 1.98 us  [pack(): pl.pallas_call(functools.partial(pack_body, windows=windows, pair_most=pa...]
    pallas_call x1, Pallas kernels: 7.08 us -> 5.07 us  [place(): pl.pallas_call(functools.partial(place_body, capacity=capacity), out_shap...]
    unnamed x8 -> x12, local copies, waits for them, and re-layouts: 1.7 us -> 3.1 us
    reshape x1, local copies, waits for them, and re-layouts: 1.33 us -> 0.08 us  [on_device(): step_count.reshape(fields, 1)]
  transfers between devices with their start and end apart: 3 -> 3, of which waited for: 3 -> 2; matrix products, arithmetic and copies ran while one was open for 7% -> 7% of each run, Pallas kernels for 0% -> 0%
where the time goes in v3:
time: 95.8 us; the launch traced here: 94.4 us
  waiting for transfers between devices  52.7 us (55%)
  starting transfers between devices  16.2 us (17%)
  local copies, waits for them, and re-layouts  7.19 us (8%)
  Pallas kernels  7.04 us (7%)
  between operations  6.52 us (7%)
  other arithmetic  4.67 us (5%)
    ppermute x2, waiting for transfers between devices, passed_along(): lax.ppermute(value, axis, [(source, source + steps) for source in range(i...  38.4 us
    all_to_all x1, waiting for transfers between devices, on_device(): lax.all_to_all(sendbuf, AXES, split_axis=0, concat_axis=0, tiled=True)  14.3 us
    ppermute x2, starting transfers between devices, passed_along(): lax.ppermute(value, axis, [(source, source + steps) for source in range(i...  9.15 us
    all_to_all x1, starting transfers between devices, on_device(): lax.all_to_all(sendbuf, AXES, split_axis=0, concat_axis=0, tiled=True)  7.09 us
    pallas_call x1, Pallas kernels, place(): pl.pallas_call(functools.partial(place_body, capacity=capacity), out_shap...  5.07 us
    unnamed x12, local copies, waits for them, and re-layouts  3.1 us
    reduce_sum x1, other arithmetic, on_device(): jnp.sum(jnp.where(slots == length - 1, around[2:], 0)) * rows + edge_row  2.03 us
    pallas_call x1, Pallas kernels, pack(): pl.pallas_call(functools.partial(pack_body, windows=windows, pair_most=pa...  1.98 us
  transfers between devices with their start and end apart: 3, of which 2 were waited for; matrix products, arithmetic and copies ran while one was open for 7% of the time, Pallas kernels for 0%

profile of v3, /device:TPU:1, one launch (start us, length us, event | category | flops | bytes accessed | tf_op | source)
XLA Modules:
  0.0 94.4 jit_solution(2163985138418727514)
XLA Ops:
  0.0 0.8 reshape.30
  0.8 0.8 select_reduce_fusion.1
  1.5 0.2 fusion.2
  1.7 0.2 convert_reduce_fusion.1
  1.9 0.0 copy-start.1
  1.9 1.4 %copy-done.1 = f32[128,24,128]{2,1,0:T(8,128)S(1)} copy-done((f32[128,24,128]{2,1,0:T(8,128)S(1)}, f32[128,24,128]{2,1,0:T(8,128)}, u32[]{:S(2)}) %copy-start.1) | copy-done | bytes 1572888
  3.3 2.0 %pack.1 = f32[32,200,128]{2,1,0:T(8,128)S(1)} custom-call(s32[161]{0:T(256)S(1)} %pad_add_fusion.table, f32[128,24,128]{2,1,0:T(8,128)S(1)} %copy-done.1), custom_call_target="tpu_custom_call" | custom-call | tf_op jit(solution)/shard_map/pack/pallas_call | solution.py:57
  5.3 0.0 copy-start
  5.3 1.7 %copy-done = f32[32,200,128]{2,1,0:T(8,128)} copy-done((f32[32,200,128]{2,1,0:T(8,128)}, f32[32,200,128]{2,1,0:T(8,128)S(1)}, u32[]{:S(2)}) %copy-start) | copy-done | bytes 3276824
  7.0 0.0 copy-start.5
  7.0 0.0 copy-start.3
  7.0 0.0 copy-start.2
  7.0 0.0 copy-start.4
  7.0 7.1 %all-to-all-start = ((f32[32,200,128]{2,1,0:T(8,128)}), f32[32,200,128]{2,1,0:T(8,128)S(1)}, u32[]{:S(2)}, u32[]{:S(2)}) async-start(f32[32,200,128]{2,1,0:T(8,128)} %copy-done), calls=%async_computation | async-start | bytes 6553600 | tf_op jit(solution)/shard_map/all_to_all | solution.py:146
  14.1 0.0 copy-done.5
  14.1 0.6 dynamic_slice.12
  16.0 0.0 copy-done.3
  16.0 0.6 and_select_fusion
  16.6 0.7 fusion.9
  17.3 3.2 %collective-permute-start = (s32[]{:T(128)}, s32[]{:T(128)}, u32[]{:S(2)}, u32[]{:S(2)}) collective-permute-start(s32[]{:T(128)} %bitcast.1), channel_id=1, source_target_pairs={{0,1},{1,2},{2,3},{3,4},{4,5},{5,6},{6,7},{7,8},{8,9},{9,10},{10,1... | collective-permute-start | bytes 20 | tf_op jit(solution)/shard_map/ppermute | solution.py:18
  20.6 5.9 %collective-permute-start.1 = (s32[]{:T(128)}, s32[]{:T(128)}, u32[]{:S(2)}, u32[]{:S(2)}) collective-permute-start(s32[]{:T(128)} %bitcast.3), channel_id=1, source_target_pairs={{1,0},{2,1},{3,2},{4,3},{5,4},{6,5},{7,6},{8,7},{9,8},{10,9},{11,1... | collective-permute-start | bytes 20 | tf_op jit(solution)/shard_map/ppermute | solution.py:18
  26.5 0.6 fusion.8
  31.0 0.0 copy-done.2
  31.0 0.1 add_select_fusion.2
  31.1 0.1 slice.12
  31.2 0.5 slice.14
  31.7 0.0 copy-done.4
  31.7 0.1 copy.8.counts
  31.8 0.1 and_select_fusion.1
  31.9 0.1 convert_reduce_fusion
  32.0 2.0 %fusion.7 = (s32[]{:T(128)}, s32[256]{0:T(256)S(1)}) fusion(s32[258]{0:T(512)S(1)} %add_select_fusion.2, s32[]{:T(128)} %sub.49, s32[256]{0:T(256)S(1)} %convert_reduce_fusion, s32[]{:T(128)S(6)} %select_n.80, s32[]{:T(128)} %fusion.8, s32[]{:T(128)} %bitcast), kind=kLoop, calls=%fused_computation.35 | loop fusion | flops 6655 | bytes 4116 | tf_op jit(solution)/shard_map/reduce_sum | solution.py:166
  35.2 38.4 %collective-permute-done = s32[]{:T(128)} collective-permute-done((s32[]{:T(128)}, s32[]{:T(128)}, u32[]{:S(2)}, u32[]{:S(2)}) %collective-permute-start) | collective-permute-done | bytes 36 | tf_op jit(solution)/shard_map/ppermute | solution.py:18
  73.6 0.0 collective-permute-done.1
  73.6 1.3 %concatenate.6.info = s32[517]{0:T(1024)S(1)} concatenate(s32[256]{0:T(256)S(1)} %get-tuple-element.8, s32[256]{0:T(256)S(1)} %and_select_fusion, s32[1]{0:T(128)} %bitcast.2, s32[1]{0:T(128)} %bitcast.4, s32[1]{0:T(128)} %bitcast.5, s32[1]{0:T(128)S(6)} %add.61, s32[1]{0:T(128)} %bitcast.6), dimensions={0} | concatenate | bytes 4136 | tf_op jit(solution)/shard_map/concatenate | solution.py:168
  75.0 14.3 %all-to-all-done = f32[32,200,128]{2,1,0:T(8,128)S(1)} async-done(((f32[32,200,128]{2,1,0:T(8,128)}), f32[32,200,128]{2,1,0:T(8,128)S(1)}, u32[]{:S(2)}, u32[]{:S(2)}) %all-to-all-start) | async-done | bytes 3276832 | tf_op jit(solution)/shard_map/all_to_all | solution.py:146
  89.3 5.1 %place.1 = f32[256,24,128]{2,1,0:T(8,128)} custom-call(s32[517]{0:T(1024)S(1)} %concatenate.6.info, f32[6400,128]{1,0:T(8,128)S(1)} %bitcast.9, s32[24,1]{1,0:T(8,128)S(1)} %copy.8.counts), custom_call_target="tpu_custom_call" | custom-call | tf_op jit(solution)/shard_map/place/pallas_call | solution.py:114
  (2 shorter events, 0.0 us)
Async XLA Ops:
  1.9 1.4 %copy-start.1 = (f32[128,24,128]{2,1,0:T(8,128)S(1)}, f32[128,24,128]{2,1,0:T(8,128)}, u32[]{:S(2)}) copy-start(f32[128,24,128]{2,1,0:T(8,128)} %accum.1) | copy-start | bytes 4718596
  5.3 1.7 %copy-start = (f32[32,200,128]{2,1,0:T(8,128)}, f32[32,200,128]{2,1,0:T(8,128)S(1)}, u32[]{:S(2)}) copy-start(f32[32,200,128]{2,1,0:T(8,128)S(1)} %pack.1) | copy-start | bytes 9830404
  7.0 7.1 %copy-start.5 = (s32[32]{0:T(128)S(1)}, s32[32]{0:T(128)}, u32[]{:S(2)}) copy-start(s32[32]{0:T(128)} %param.8) | copy-start | bytes 388
  7.0 9.0 %copy-start.3 = (s32[256]{0:T(256)S(1)}, s32[256]{0:T(256)}, u32[]{:S(2)}) copy-start(s32[256]{0:T(256)} %param.9) | copy-start | bytes 3076
  7.0 24.0 %copy-start.2 = (s32[4096]{0:T(1024)S(1)}, s32[4096]{0:T(1024)}, u32[]{:S(2)}) copy-start(s32[4096]{0:T(1024)} %param.7) | copy-start | bytes 49156
  7.0 24.7 %copy-start.4 = (s32[24]{0:T(128)S(1)}, s32[24]{0:T(128)}, u32[]{:S(2)}) copy-start(s32[24]{0:T(128)} %param.6) | copy-start | bytes 292
  7.0 82.3 %all-to-all-start = ((f32[32,200,128]{2,1,0:T(8,128)}), f32[32,200,128]{2,1,0:T(8,128)S(1)}, u32[]{:S(2)}, u32[]{:S(2)}) async-start(f32[32,200,128]{2,1,0:T(8,128)} %copy-done), calls=%async_computation | async-start | bytes 6553600 | tf_op jit(solution)/shard_map/all_to_all | solution.py:146
  17.3 56.3 %collective-permute-start = (s32[]{:T(128)}, s32[]{:T(128)}, u32[]{:S(2)}, u32[]{:S(2)}) collective-permute-start(s32[]{:T(128)} %bitcast.1), channel_id=1, source_target_pairs={{0,1},{1,2},{2,3},{3,4},{4,5},{5,6},{6,7},{7,8},{8,9},{9,10},{10,1... | collective-permute-start | bytes 20 | tf_op jit(solution)/shard_map/ppermute | solution.py:18
  20.6 53.1 %collective-permute-start.1 = (s32[]{:T(128)}, s32[]{:T(128)}, u32[]{:S(2)}, u32[]{:S(2)}) collective-permute-start(s32[]{:T(128)} %bitcast.3), channel_id=1, source_target_pairs={{1,0},{2,1},{3,2},{4,3},{5,4},{6,5},{7,6},{8,7},{9,8},{10,9},{11,1... | collective-permute-start | bytes 20 | tf_op jit(solution)/shard_map/ppermute | solution.py:18

commit v4 on v3

--- a/solution.py
+++ b/solution.py
@@ -53,10 +53,10 @@
 def pack(table, accum, windows, owners, pair_most):
     blocks, fields, cells = accum.shape
     rows = pair_most * fields + TILE
-    steps = 8
+    steps = 4
     return pl.pallas_call(
         functools.partial(pack_body, windows=windows, pair_most=pair_most),
-        out_shape=jax.ShapeDtypeStruct((owners, rows, cells), jnp.float32),
+        out_shape=pltpu.HBM((owners, rows, cells), jnp.float32),
         grid=(steps,),
         in_specs=[
             pl.BlockSpec(memory_space=pltpu.SMEM),
@@ -108,7 +108,7 @@
 
 
 def place(info, received, counts, capacity, fields, cells):
-    steps = 8
+    steps = 4
     chunk = capacity // steps
     whole = pl.BlockSpec(memory_space=pltpu.VMEM)
     return pl.pallas_call(

time: 95.8 us -> 94.3 us (0.984)
  local copies, waits for them, and re-layouts: 7.19 us -> 5.51 us
    unnamed x12 -> x10, local copies, waits for them, and re-layouts: 3.1 us -> 1.42 us
    pallas_call x1, Pallas kernels: 1.98 us -> 3.4 us  [pack(): pl.pallas_call(functools.partial(pack_body, windows=windows, pair_most=pa...]
    pallas_call x1, Pallas kernels: 5.07 us -> 3.85 us  [place(): pl.pallas_call(functools.partial(place_body, capacity=capacity), out_shap...]
where the time goes in v4:
time: 94.3 us; the launch traced here: 92.9 us
  waiting for transfers between devices  52.7 us (56%)
  starting transfers between devices  16.2 us (17%)
  Pallas kernels  7.25 us (8%)
  between operations  6.51 us (7%)
  local copies, waits for them, and re-layouts  5.51 us (6%)
  other arithmetic  4.67 us (5%)
    ppermute x2, waiting for transfers between devices, passed_along(): lax.ppermute(value, axis, [(source, source + steps) for source in range(i...  38.4 us
    all_to_all x1, waiting for transfers between devices, on_device(): lax.all_to_all(sendbuf, AXES, split_axis=0, concat_axis=0, tiled=True)  14.3 us
    ppermute x2, starting transfers between devices, passed_along(): lax.ppermute(value, axis, [(source, source + steps) for source in range(i...  9.15 us
    all_to_all x1, starting transfers between devices, on_device(): lax.all_to_all(sendbuf, AXES, split_axis=0, concat_axis=0, tiled=True)  7.09 us
    pallas_call x1, Pallas kernels, place(): pl.pallas_call(functools.partial(place_body, capacity=capacity), out_shap...  3.85 us
    pallas_call x1, Pallas kernels, pack(): pl.pallas_call(functools.partial(pack_body, windows=windows, pair_most=pa...  3.4 us
    reduce_sum x1, other arithmetic, on_device(): jnp.sum(jnp.where(slots == length - 1, around[2:], 0)) * rows + edge_row  2.03 us
  transfers between devices with their start and end apart: 3, of which 2 were waited for; matrix products, arithmetic and copies ran while one was open for 7% of the time, Pallas kernels for 0%

profile of v4, /device:TPU:1, one launch (start us, length us, event | category | flops | bytes accessed | tf_op | source)
XLA Modules:
  0.0 92.9 jit_solution(7797775015514591372)
XLA Ops:
  0.0 0.8 reshape.30
  0.8 0.8 select_reduce_fusion.1
  1.5 0.2 fusion.2
  1.7 0.2 convert_reduce_fusion.1
  1.9 0.0 copy-start
  1.9 1.4 %copy-done = f32[128,24,128]{2,1,0:T(8,128)S(1)} copy-done((f32[128,24,128]{2,1,0:T(8,128)S(1)}, f32[128,24,128]{2,1,0:T(8,128)}, u32[]{:S(2)}) %copy-start) | copy-done | bytes 1572888
  3.3 3.4 %pack.1 = f32[32,200,128]{2,1,0:T(8,128)} custom-call(s32[161]{0:T(256)S(1)} %pad_add_fusion.table, f32[128,24,128]{2,1,0:T(8,128)S(1)} %copy-done), custom_call_target="tpu_custom_call" | custom-call | tf_op jit(solution)/shard_map/pack/pallas_call | solution.py:57
  6.7 0.0 copy-start.4
  6.7 0.0 copy-start.2
  6.7 0.0 copy-start.1
  6.7 0.0 copy-start.3
  6.7 7.1 %all-to-all-start = ((f32[32,200,128]{2,1,0:T(8,128)}), f32[32,200,128]{2,1,0:T(8,128)S(1)}, u32[]{:S(2)}, u32[]{:S(2)}) async-start(f32[32,200,128]{2,1,0:T(8,128)} %pack.1), calls=%async_computation | async-start | bytes 6553600 | tf_op jit(solution)/shard_map/all_to_all | solution.py:146
  13.8 0.0 copy-done.4
  13.8 0.6 dynamic_slice.12
  15.7 0.0 copy-done.2
  15.7 0.6 and_select_fusion
  16.4 0.7 fusion.9
  17.0 3.2 %collective-permute-start = (s32[]{:T(128)}, s32[]{:T(128)}, u32[]{:S(2)}, u32[]{:S(2)}) collective-permute-start(s32[]{:T(128)} %bitcast.1), channel_id=1, source_target_pairs={{0,1},{1,2},{2,3},{3,4},{4,5},{5,6},{6,7},{7,8},{8,9},{9,10},{10,1... | collective-permute-start | bytes 20 | tf_op jit(solution)/shard_map/ppermute | solution.py:18
  20.3 5.9 %collective-permute-start.1 = (s32[]{:T(128)}, s32[]{:T(128)}, u32[]{:S(2)}, u32[]{:S(2)}) collective-permute-start(s32[]{:T(128)} %bitcast.3), channel_id=1, source_target_pairs={{1,0},{2,1},{3,2},{4,3},{5,4},{6,5},{7,6},{8,7},{9,8},{10,9},{11,1... | collective-permute-start | bytes 20 | tf_op jit(solution)/shard_map/ppermute | solution.py:18
  26.2 0.6 fusion.8
  30.7 0.0 copy-done.1
  30.7 0.1 add_select_fusion.2
  30.8 0.1 slice.12
  30.9 0.5 slice.14
  31.4 0.0 copy-done.3
  31.4 0.1 copy.8.counts
  31.5 0.1 and_select_fusion.1
  31.6 0.1 convert_reduce_fusion
  31.7 2.0 %fusion.7 = (s32[]{:T(128)}, s32[256]{0:T(256)S(1)}) fusion(s32[258]{0:T(512)S(1)} %add_select_fusion.2, s32[]{:T(128)} %sub.49, s32[256]{0:T(256)S(1)} %convert_reduce_fusion, s32[]{:T(128)S(6)} %select_n.80, s32[]{:T(128)} %fusion.8, s32[]{:T(128)} %bitcast), kind=kLoop, calls=%fused_computation.35 | loop fusion | flops 6655 | bytes 4116 | tf_op jit(solution)/shard_map/reduce_sum | solution.py:166
  35.0 38.4 %collective-permute-done = s32[]{:T(128)} collective-permute-done((s32[]{:T(128)}, s32[]{:T(128)}, u32[]{:S(2)}, u32[]{:S(2)}) %collective-permute-start) | collective-permute-done | bytes 36 | tf_op jit(solution)/shard_map/ppermute | solution.py:18
  73.4 0.0 collective-permute-done.1
  73.4 1.3 %concatenate.6.info = s32[517]{0:T(1024)S(1)} concatenate(s32[256]{0:T(256)S(1)} %get-tuple-element.8, s32[256]{0:T(256)S(1)} %and_select_fusion, s32[1]{0:T(128)} %bitcast.2, s32[1]{0:T(128)} %bitcast.4, s32[1]{0:T(128)} %bitcast.5, s32[1]{0:T(128)S(6)} %add.61, s32[1]{0:T(128)} %bitcast.6), dimensions={0} | concatenate | bytes 4136 | tf_op jit(solution)/shard_map/concatenate | solution.py:168
  74.7 14.3 %all-to-all-done = f32[32,200,128]{2,1,0:T(8,128)S(1)} async-done(((f32[32,200,128]{2,1,0:T(8,128)}), f32[32,200,128]{2,1,0:T(8,128)S(1)}, u32[]{:S(2)}, u32[]{:S(2)}) %all-to-all-start) | async-done | bytes 3276832 | tf_op jit(solution)/shard_map/all_to_all | solution.py:146
  89.0 3.8 %place.1 = f32[256,24,128]{2,1,0:T(8,128)} custom-call(s32[517]{0:T(1024)S(1)} %concatenate.6.info, f32[6400,128]{1,0:T(8,128)S(1)} %bitcast.9, s32[24,1]{1,0:T(8,128)S(1)} %copy.8.counts), custom_call_target="tpu_custom_call" | custom-call | tf_op jit(solution)/shard_map/place/pallas_call | solution.py:114
  (2 shorter events, 0.0 us)
Async XLA Ops:
  1.9 1.4 %copy-start = (f32[128,24,128]{2,1,0:T(8,128)S(1)}, f32[128,24,128]{2,1,0:T(8,128)}, u32[]{:S(2)}) copy-start(f32[128,24,128]{2,1,0:T(8,128)} %accum.1) | copy-start | bytes 4718596
  6.7 7.1 %copy-start.4 = (s32[32]{0:T(128)S(1)}, s32[32]{0:T(128)}, u32[]{:S(2)}) copy-start(s32[32]{0:T(128)} %param.8) | copy-start | bytes 388
  6.7 9.0 %copy-start.2 = (s32[256]{0:T(256)S(1)}, s32[256]{0:T(256)}, u32[]{:S(2)}) copy-start(s32[256]{0:T(256)} %param.9) | copy-start | bytes 3076
  6.7 24.0 %copy-start.1 = (s32[4096]{0:T(1024)S(1)}, s32[4096]{0:T(1024)}, u32[]{:S(2)}) copy-start(s32[4096]{0:T(1024)} %param.7) | copy-start | bytes 49156
  6.7 24.7 %copy-start.3 = (s32[24]{0:T(128)S(1)}, s32[24]{0:T(128)}, u32[]{:S(2)}) copy-start(s32[24]{0:T(128)} %param.6) | copy-start | bytes 292
  6.7 82.3 %all-to-all-start = ((f32[32,200,128]{2,1,0:T(8,128)}), f32[32,200,128]{2,1,0:T(8,128)S(1)}, u32[]{:S(2)}, u32[]{:S(2)}) async-start(f32[32,200,128]{2,1,0:T(8,128)} %pack.1), calls=%async_computation | async-start | bytes 6553600 | tf_op jit(solution)/shard_map/all_to_all | solution.py:146
  17.0 56.3 %collective-permute-start = (s32[]{:T(128)}, s32[]{:T(128)}, u32[]{:S(2)}, u32[]{:S(2)}) collective-permute-start(s32[]{:T(128)} %bitcast.1), channel_id=1, source_target_pairs={{0,1},{1,2},{2,3},{3,4},{4,5},{5,6},{6,7},{7,8},{8,9},{9,10},{10,1... | collective-permute-start | bytes 20 | tf_op jit(solution)/shard_map/ppermute | solution.py:18
  20.3 53.1 %collective-permute-start.1 = (s32[]{:T(128)}, s32[]{:T(128)}, u32[]{:S(2)}, u32[]{:S(2)}) collective-permute-start(s32[]{:T(128)} %bitcast.3), channel_id=1, source_target_pairs={{1,0},{2,1},{3,2},{4,3},{5,4},{6,5},{7,6},{8,7},{9,8},{10,9},{11,1... | collective-permute-start | bytes 20 | tf_op jit(solution)/shard_map/ppermute | solution.py:18
